TPU v7x, 128 devices: a whole 4x4x4 slice. The times are simulated.
128 devices in a mesh: section: 2 (over x_hi), grp: 64 (over y, z, x_lo, core).
Axes of the slice: x: 4 (x_hi: 2, x_lo: 2; x = x_hi * 2 + x_lo), y: 4, z: 4, core: 2. Of those that a mesh axis runs over, the one named last changes fastest.
Arguments:
- voltages: bfloat16 [1024, 524288], P('grp', 'section'), may hold values from -6 to 6
- filter_taps: float32 [8, 512], replicated, may hold values from -2 to 2
- beam_weights: bfloat16 [256, 2, 512, 1024], P('grp'), may hold values from -0.125 to 0.125
- antenna_of_row: int32 [1024], replicated, may hold values from 0 to 1023, each once
- beam_delay: int32 [512], P('grp'), may hold values from 0 to 127
Outputs:
- dedispersed: float32 [256, 2, 512, 1024], P(None, None, 'grp', 'section')
Inputs may be any that keep to these rules, and one draw needn't show every extreme that they name: A permutation: voltage row r holds physical antenna antenna_of_row[r].
All inputs are finite; a program needn't handle non-finite values.
Results may differ from a plain program's by a relative error of at most 0.0069.
Values may be sent and summed in bfloat16 or wider, within the bound.
A program may use at most 128 MiB of HBM per device.

v0:
```python
import math
import jax
import jax.numpy as jnp
from jax import lax
from jax.sharding import PartitionSpec as P

DFT_LEN = 256


def shifted(value, axis, steps):
    count = lax.axis_size(axis)
    leading, last = (max(0, -steps), min(count, count - steps))
    return lax.ppermute(value, axis, [(source, source + steps) for source in range(leading, last)])


def dft_table(frame_length, group_count, split_ways):
    channels = frame_length // 2
    per_target = channels // (group_count * split_ways)
    column = jnp.arange(frame_length, dtype=jnp.int32)
    target = column // (2 * per_target)
    within = column % (2 * per_target)
    quadrature = within // per_target
    channel = (
        target % group_count * (per_target * split_ways)
        + target // group_count * per_target
        + within % per_target
    )
    sample = jnp.arange(frame_length, dtype=jnp.int32)[:, None]
    winding = sample * channel[None, :] % frame_length
    angles = 2.0 * math.pi / frame_length * winding.astype(jnp.float32)
    factor = channels ** (-0.5)
    dft_cols = jnp.where(
        quadrature[None, :] == 0, jnp.cos(angles) * factor, -jnp.sin(angles) * factor
    )
    return dft_cols.astype(jnp.bfloat16)


def block_tables(length):
    half_len = length // 2
    factor = length ** (-0.5)
    sample = jnp.arange(length, dtype=jnp.int32)
    angles = (
        2.0 * math.pi / length * (sample[:, None] * sample[None, :] % length).astype(jnp.float32)
    )
    cosine_table = (jnp.cos(angles) * factor).astype(jnp.bfloat16)
    sine_table = (jnp.sin(angles) * factor).astype(jnp.bfloat16)
    forward_real = jnp.concatenate([cosine_table, -sine_table], axis=1)
    forward_imag = jnp.concatenate([sine_table, cosine_table], axis=1)
    back_cos = cosine_table[:, half_len:]
    back_sin = sine_table[:, half_len:]
    inverse_real = jnp.concatenate([back_cos, back_sin], axis=1)
    inverse_imag = jnp.concatenate([-back_sin, back_cos], axis=1)
    return (forward_real, forward_imag, inverse_real, inverse_imag)


def chirp_factor(delays, channel_count, channels, length):
    frequency = jnp.arange(length, dtype=jnp.int32)
    signed = jnp.where(frequency < length // 2, frequency, frequency - length).astype(jnp.float32)
    channel = jnp.arange(channel_count, dtype=jnp.int32).astype(jnp.float32)
    strength = (1.0 + channel / channels) ** (-3.0)
    sweep = signed * signed / (length * length)
    phases = (math.pi * delays.astype(jnp.float32))[None, :, None] * strength[
        :, None, None
    ] * sweep[None, None, :] - 0.5 * math.pi * frequency.astype(jnp.float32)[None, None, :]
    return (jnp.cos(phases), jnp.sin(phases))


def dedisperse(series, leading, delays, tables, channels):
    forward_real, forward_imag, inverse_real, inverse_imag = tables
    length = forward_real.shape[0]
    advance = length // 2
    chan_count = series.shape[0]
    beam_count = series.shape[2]
    time_len = series.shape[3]
    block_count = time_len // advance
    joined = jnp.concatenate([leading, series], axis=3).reshape(
        chan_count, 2, beam_count, block_count + 1, advance
    )
    blocks = jnp.concatenate([joined[:, :, :, :-1, :], joined[:, :, :, 1:, :]], axis=4)
    spectrum = jnp.einsum(
        "cbml,lk->cbmk", blocks[:, 0], forward_real, preferred_element_type=jnp.float32
    ) + jnp.einsum("cbml,lk->cbmk", blocks[:, 1], forward_imag, preferred_element_type=jnp.float32)
    chirp_real, chirp_imag = chirp_factor(delays, chan_count, channels, length)
    chirp_real = chirp_real[:, :, None, :]
    chirp_imag = chirp_imag[:, :, None, :]
    spec_real = spectrum[..., :length]
    spec_imag = spectrum[..., length:]
    filtered_real = (spec_real * chirp_real - spec_imag * chirp_imag).astype(jnp.bfloat16)
    filtered_imag = (spec_real * chirp_imag + spec_imag * chirp_real).astype(jnp.bfloat16)
    result = jnp.einsum(
        "cbmk,kn->cbmn", filtered_real, inverse_real, preferred_element_type=jnp.float32
    ) + jnp.einsum("cbmk,kn->cbmn", filtered_imag, inverse_imag, preferred_element_type=jnp.float32)
    out_real = result[..., :advance].reshape(chan_count, beam_count, time_len)
    out_imag = result[..., advance:].reshape(chan_count, beam_count, time_len)
    return jnp.stack([out_real, out_imag], axis=1)


def local(voltages, filter_taps, beam_weights, antenna_of_row, beam_delay):
    group_count = lax.axis_size("grp")
    antenna_row_set = voltages.shape[0]
    samples = voltages.shape[1]
    filter_tap_count = filter_taps.shape[0]
    frame_length = filter_taps.shape[1]
    channel_spectra = samples // frame_length
    channels = frame_length // 2
    antennas = antenna_of_row.shape[0]
    beam_count = beam_weights.shape[2]
    past_samples = shifted(
        voltages[:, samples - (filter_tap_count - 1) * frame_length :], "section", 1
    )
    extended = jnp.concatenate([past_samples, voltages], axis=1).reshape(
        antenna_row_set, channel_spectra + filter_tap_count - 1, frame_length
    )
    weighted = filter_taps[0] * extended[:, 0:channel_spectra, :]
    for tap_index in range(1, filter_tap_count):
        weighted = (
            weighted
            + filter_taps[tap_index] * extended[:, tap_index : tap_index + channel_spectra, :]
        )
    weighted = weighted.astype(jnp.bfloat16)
    split_ways = 1
    dft_cols = dft_table(frame_length, group_count, split_ways)
    channelised = jnp.einsum(
        "asp,pj->ajs", weighted, dft_cols, preferred_element_type=jnp.float32
    ).astype(jnp.bfloat16)[None]
    per_target = channels // (group_count * split_ways)
    ordered = jnp.take(beam_weights, antenna_of_row, axis=3).reshape(
        per_target, 2 * beam_count, antennas
    )
    tables = block_tables(DFT_LEN)
    received = lax.all_to_all(channelised, "grp", split_axis=2, concat_axis=0, tiled=True)
    item_count = received.shape[3]
    halves = received.shape[0] * received.shape[1] // antennas
    all_rows = received.reshape(halves, antennas, 2 * per_target, item_count)
    with_real = jnp.einsum(
        "cba,hacs->cbhs",
        ordered,
        all_rows[:, :, :per_target, :],
        preferred_element_type=jnp.float32,
    )
    with_imag = jnp.einsum(
        "cba,hacs->cbhs",
        ordered,
        all_rows[:, :, per_target:, :],
        preferred_element_type=jnp.float32,
    )
    beam_real = with_real[:, :beam_count] - with_imag[:, beam_count:]
    beam_imag = with_imag[:, :beam_count] + with_real[:, beam_count:]
    formed = jnp.stack([beam_real, beam_imag], axis=1).astype(jnp.bfloat16)
    arrival_buffer = lax.all_to_all(
        formed.reshape(per_target, 2, beam_count, channel_spectra),
        "grp",
        split_axis=2,
        concat_axis=0,
        tiled=True,
    )
    leading = shifted(arrival_buffer[:, :, :, channel_spectra - DFT_LEN // 2 :], "section", 1)
    result = dedisperse(arrival_buffer, leading, beam_delay, tables, channels)
    return result


def solution(mesh):
    in_specs = (P("grp", "section"), P(), P("grp", None, None, None), P(), P("grp"))
    out_specs = P(None, None, "grp", "section")
    return jax.shard_map(local, mesh=mesh, in_specs=in_specs, out_specs=out_specs, check_vma=False)
```

profile of v0, /device:TPU:70, one launch (start us, length us, event | category | flops | bytes accessed | tf_op | source)
XLA Modules:
  0.0 427.6 jit_solution(12808330259375173368)
XLA Ops:
  9.2 7.2 %pad_maximum_fusion = bf16[16,265728]{1,0:T(8,128)(2,1)} fusion(bf16[16,262144]{1,0:T(8,128)(2,1)} %param.5, bf16[16,3584]{1,0:T(8,128)(2,1)S(1)} %collective-permute-done), kind=kLoop, calls=%fused_computation.3 | loop fusion | flops 17006592 | bytes 17006592 | tf_op jit(solution)/shard_map/concatenate | solution.py:111
  16.4 12.4 %reshape.188 = bf16[16,519,512]{2,1,0:T(8,128)(2,1)} reshape(bf16[16,265728]{1,0:T(8,128)(2,1)} %pad_maximum_fusion) | data formatting | bytes 17006592 | tf_op jit(solution)/shard_map/reshape | solution.py:111
  28.7 44.7 %convert_bitcast_fusion = bf16[1,16,512,512]{3,2,1,0:T(8,128)(2,1)} fusion(bf16[16,519,512]{2,1,0:T(8,128)(2,1)} %reshape.188, f32[512]{0:T(512)S(1)} %bitcast.97, f32[512]{0:T(512)S(1)} %bitcast.98, f32[512]{0:T(512)S(1)} %bitcast.92, f32[512]{0:T(512)S(1)} %bitcast.93, f32[512]{0:T(512)S(1)} %bitcast.94, f32[512]{0:T(512)S(1)} %bitcast.95, ...), kind=kOutput, calls=%fused_computation.8 | convolution fusion | flops 4399824896 | bytes 76038144 | tf_op jit(solution)/shard_map/asp,pj->ajs/dot_general | solution.py:123
  73.4 11.4 %copy.43 = bf16[1,16,512,512]{3,1,0,2:T(8,128)(2,1)} copy(bf16[1,16,512,512]{3,2,1,0:T(8,128)(2,1)} %convert_bitcast_fusion) | data formatting | bytes 16777216 | tf_op jit(solution)/shard_map/broadcast_in_dim | solution.py:123
  84.8 9.8 %all-to-all-start = ((bf16[1,16,512,512]{3,1,0,2:T(8,128)(2,1)}), bf16[1,16,512,512]{3,1,0,2:T(8,128)(2,1)}, u32[]{:S(2)}, u32[]{:S(2)}) async-start(bf16[1,16,512,512]{3,1,0,2:T(8,128)(2,1)} %copy.43), calls=%async_computation | async-start | bytes 16777216 | tf_op jit(solution)/shard_map/all_to_all | solution.py:131
  94.6 14.8 %copy.41 = bf16[4,2,512,1024]{2,0,3,1:T(4,128)(2,1)} copy(bf16[4,2,512,1024]{3,2,1,0:T(8,128)(2,1)} %param.7) | data formatting | bytes 16777216 | tf_op args[2]
  109.4 19.0 %gather_fusion = bf16[1024,4,2,512]{3,1,2,0:T(4,128)(2,1)} fusion(bf16[4,2,512,1024]{2,0,3,1:T(4,128)(2,1)} %copy.41, s32[1024]{0:T(1024)S(1)} %fusion.49), kind=kCustom, calls=%fused_computation | custom fusion | bytes 16781312 | tf_op jit(solution)/shard_map/jit(_take)/gather | solution.py:127
  128.4 13.7 %copy.42 = bf16[4,2,512,1024]{3,2,1,0:T(8,128)(2,1)} copy(bf16[4,2,512,1024]{2,0,1,3:T(4,128)(2,1)} %bitcast.81) | data formatting | bytes 16777216 | tf_op jit(solution)/shard_map/jit(_take)/gather | solution.py:127
  142.1 7.3 %bitcast_select_fusion = bf16[4,1024,1024]{2,1,0:T(8,128)(2,1)} fusion(bf16[4,2,512,1024]{3,2,1,0:T(8,128)(2,1)} %copy.42, pred[1024]{0:T(1024)(128)(4,1)S(1)} %compare_and_fusion), kind=kLoop, calls=%fused_computation.5 | loop fusion | flops 4194304 | bytes 16778240 | tf_op jit(solution)/shard_map/jit(_take)/select_n | solution.py:127
  149.4 62.7 %all-to-all-done = bf16[1,16,512,512]{3,1,0,2:T(8,128)(2,1)} async-done(((bf16[1,16,512,512]{3,1,0,2:T(8,128)(2,1)}), bf16[1,16,512,512]{3,1,0,2:T(8,128)(2,1)}, u32[]{:S(2)}, u32[]{:S(2)}) %all-to-all-start) | async-done | bytes 8388640 | tf_op jit(solution)/shard_map/all_to_all | solution.py:131
  212.1 8.3 %copy.44 = bf16[1,16,64,8,512]{4,1,2,3,0:T(8,128)(2,1)} copy(bf16[1,16,64,8,512]{4,1,3,2,0:T(8,128)(2,1)} %bitcast.13) | data formatting | bytes 16777216 | tf_op jit(solution)/shard_map/all_to_all | solution.py:131
  220.5 8.3 %fusion.12 = f32[4,1024,1,512]{3,1,0,2:T(8,128)S(1)} fusion(bf16[4,1024,1024]{2,1,0:T(8,128)(2,1)} %bitcast_select_fusion, bf16[1,1024,8,512]{3,1,2,0:T(8,128)(2,1)} %bitcast.89), kind=kOutput, calls=%fused_computation.32 | convolution fusion | flops 4294967296 | bytes 20971520 | tf_op jit(solution)/shard_map/cba,hacs->cbhs/dot_general | solution.py:135
  228.8 9.0 %fusion.13 = f32[4,1024,1,512]{3,1,0,2:T(8,128)} fusion(bf16[4,1024,1024]{2,1,0:T(8,128)(2,1)S(1)} %bitcast.88, bf16[1,1024,8,512]{3,1,2,0:T(8,128)(2,1)} %bitcast.90), kind=kOutput, calls=%fused_computation.33 | convolution fusion | flops 4294967296 | bytes 20971520 | tf_op jit(solution)/shard_map/cba,hacs->cbhs/dot_general | solution.py:141
  247.7 9.0 %all-to-all-start.1 = ((bf16[4,2,512,512]{3,0,1,2:T(4,128)(2,1)}), bf16[4,2,512,512]{3,0,1,2:T(4,128)(2,1)}, u32[]{:S(2)}, u32[]{:S(2)}) async-start(bf16[4,2,512,512]{3,0,1,2:T(4,128)(2,1)} %copy.45), calls=%async_computation.1 | async-start | bytes 8388608 | tf_op jit(solution)/shard_map/all_to_all | solution.py:150
  258.8 52.8 %all-to-all-done.1 = bf16[4,2,512,512]{3,0,1,2:T(4,128)(2,1)} async-done(((bf16[4,2,512,512]{3,0,1,2:T(4,128)(2,1)}), bf16[4,2,512,512]{3,0,1,2:T(4,128)(2,1)}, u32[]{:S(2)}, u32[]{:S(2)}) %all-to-all-start.1) | async-done | bytes 4194336 | tf_op jit(solution)/shard_map/all_to_all | solution.py:150
  317.5 7.4 %fusion.18 = (f32[256,8,256]{2,0,1:T(8,128)S(1)}, f32[256,8,256]{2,0,1:T(8,128)S(1)}) fusion(f32[256]{0:T(256)S(1)} %get-tuple-element.26, f32[256]{0:T(256)S(1)} %get-tuple-element.25, f32[256,8]{0,1:T(8,128)S(1)} %broadcast_multiply_fusion), kind=kLoop, calls=%fused_computation.39 | loop fusion | flops 1048576 | bytes 4204544 | tf_op jit(solution)/shard_map/cos | solution.py:65
  324.9 19.2 %collective-permute-done.1 = bf16[256,2,8,128]{3,2,1,0:T(8,128)(2,1)S(1)} collective-permute-done((bf16[256,2,8,128]{3,2,1,0:T(8,128)(2,1)S(1)}, bf16[256,2,8,128]{3,2,1,0:T(8,128)(2,1)S(1)}, u32[]{:S(2)}, u32[]{:S(2)}) %collective-permute-start.1) | collective-permute-done | bytes 1048608 | tf_op jit(solution)/shard_map/ppermute | solution.py:13
  353.9 8.1 %fusion.3 = f32[256,8,4,512]{3,0,2,1:T(8,128)} fusion(bf16[256,2,8,4,256]{4,0,3,2,1:T(8,128)(2,1)S(1)} %copy_dynamic-update-slice_fusion, bf16[256,256]{1,0:T(8,128)(2,1)S(1)} %fusion.48, bf16[256,256]{1,0:T(8,128)(2,1)S(1)} %get-tuple-element.24), kind=kOutput, calls=%fused_computation.15 | convolution fusion | flops 2148007936 | bytes 21233664 | tf_op jit(solution)/shard_map/cbml,lk->cbmk/dot_general | solution.py:80
  362.0 13.9 %convolution_add_fusion = f32[256,8,4,512]{3,0,2,1:T(8,128)} fusion(f32[256,8,4,512]{3,0,2,1:T(8,128)} %fusion.3, bf16[256,2,8,4,256]{4,0,3,2,1:T(8,128)(2,1)S(1)} %copy_dynamic-update-slice_fusion, bf16[256,256]{1,0:T(8,128)(2,1)S(1)} %get-tuple-element.24, bf16[256,256]{1,0:T(8,128)(2,1)S(1)} %get-tuple-element.23), kind=kOutput, calls=%fused_computation.2 | convolution fusion | flops 2152202240 | bytes 38010880 | tf_op jit(solution)/shard_map/cbml,lk->cbmk/dot_general | solution.py:82
  375.9 10.9 %fusion.1 = f32[256,8,4,256]{0,3,2,1:T(8,128)} fusion(f32[256,8,4,512]{3,0,2,1:T(8,128)} %convolution_add_fusion, f32[256,8,256]{2,0,1:T(8,128)S(1)} %get-tuple-element.22, f32[256,8,256]{2,0,1:T(8,128)S(1)} %get-tuple-element.21, bf16[256,128]{1,0:T(8,128)(2,1)S(1)} %get-tuple-element.12, bf16[256,128]{1,0:T(8,128)(2,1)S(1)} %slice.163), kind=kOutput, calls=%fused_computation.11 | convolution fusion | flops 1082392576 | bytes 29491200 | tf_op jit(solution)/shard_map/cbmk,kn->cbmn/dot_general | solution.py:90
  386.8 13.5 %fusion.14 = f32[256,8,4,256]{0,3,2,1:T(8,128)} fusion(f32[256,8,4,256]{0,3,2,1:T(8,128)} %fusion.1, f32[256,8,4,512]{3,0,2,1:T(8,128)} %convolution_add_fusion, f32[256,8,256]{2,0,1:T(8,128)S(1)} %get-tuple-element.22, f32[256,8,256]{2,0,1:T(8,128)S(1)} %get-tuple-element.21, bf16[256,128]{1,0:T(8,128)(2,1)S(1)} %slice.163, ...), kind=kOutput, calls=%fused_computation.34 | convolution fusion | flops 1084489728 | bytes 37879808 | tf_op jit(solution)/shard_map/cbmk,kn->cbmn/dot_general | solution.py:92
  400.2 7.7 %fusion.78 = (f32[256,8,4,128]{0,3,2,1:T(8,128)}, f32[256,8,4,128]{0,3,2,1:T(8,128)}) fusion(f32[256,8,4,256]{0,3,2,1:T(8,128)} %fusion.14), kind=kLoop, calls=%fused_computation.136 | loop fusion | bytes 16777216 | tf_op jit(solution)/shard_map/slice | solution.py:93
  407.9 5.6 %copy.52 = f32[256,1,8,512]{3,2,1,0:T(8,128)} copy(f32[256,1,8,512]{0,3,2,1:T(8,128)} %bitcast.86) | data formatting | bytes 8388608 | tf_op jit(solution)/shard_map/stack;reshape | solution.py:95
  419.1 8.1 %pad_maximum_fusion.1 = f32[256,2,8,512]{3,2,1,0:T(8,128)} fusion(f32[256,1,8,512]{3,2,1,0:T(8,128)} %copy.53, f32[256,1,8,512]{3,2,1,0:T(8,128)} %copy.52), kind=kLoop, calls=%fused_computation.4 | loop fusion | flops 2097152 | bytes 16777216 | tf_op jit(solution)/shard_map/stack | solution.py:95
  (38 shorter events, 42.3 us)
Async XLA Ops:
  0.9 8.3 %collective-permute-start = (bf16[16,3584]{1,0:T(8,128)(2,1)S(1)}, bf16[16,3584]{1,0:T(8,128)(2,1)S(1)}, u32[]{:S(2)}, u32[]{:S(2)}) collective-permute-start(bf16[16,3584]{1,0:T(8,128)(2,1)S(1)} %slice.107), channel_id=1, source_target_pairs={{0,64},{1,65},{2,66},{3,67},{4,68},{5,69},{6,70},{7,71},{8,72},{9,... | collective-permute-start | bytes 344072 | tf_op jit(solution)/shard_map/ppermute | solution.py:13
  84.8 127.4 %all-to-all-start = ((bf16[1,16,512,512]{3,1,0,2:T(8,128)(2,1)}), bf16[1,16,512,512]{3,1,0,2:T(8,128)(2,1)}, u32[]{:S(2)}, u32[]{:S(2)}) async-start(bf16[1,16,512,512]{3,1,0,2:T(8,128)(2,1)} %copy.43), calls=%async_computation | async-start | bytes 16777216 | tf_op jit(solution)/shard_map/all_to_all | solution.py:131
  94.6 14.8 %copy-start = (s32[1024]{0:T(1024)S(1)}, s32[1024]{0:T(1024)}, u32[]{:S(2)}) copy-start(s32[1024]{0:T(1024)} %param.8) | copy-start | bytes 12292
  212.1 16.6 %slice-start = ((s8[8388608]{0:T(1024)(128)(4,1)}), s8[4194304]{0:T(1024)(128)(4,1)S(1)}, s32[]{:S(2)}) async-start(s8[8388608]{0:T(1024)(128)(4,1)} %bitcast.87), calls=%async_computation.2 | async-start | bytes 8388608
  220.5 8.3 %slice-start.1 = ((s8[8388608]{0:T(1024)(128)(4,1)}), s8[4194304]{0:T(1024)(128)(4,1)S(1)}, s32[]{:S(2)}) async-start(s8[8388608]{0:T(1024)(128)(4,1)} %bitcast.87), calls=%async_computation.3 | async-start | bytes 8388608
  247.7 64.0 %all-to-all-start.1 = ((bf16[4,2,512,512]{3,0,1,2:T(4,128)(2,1)}), bf16[4,2,512,512]{3,0,1,2:T(4,128)(2,1)}, u32[]{:S(2)}, u32[]{:S(2)}) async-start(bf16[4,2,512,512]{3,0,1,2:T(4,128)(2,1)} %copy.45), calls=%async_computation.1 | async-start | bytes 8388608 | tf_op jit(solution)/shard_map/all_to_all | solution.py:150
  258.8 58.5 %copy-start.1 = (s32[8]{0:T(128)S(1)}, s32[8]{0:T(128)}, u32[]{:S(2)}) copy-start(s32[8]{0:T(128)} %param.9) | copy-start | bytes 100
  316.0 28.0 %collective-permute-start.1 = (bf16[256,2,8,128]{3,2,1,0:T(8,128)(2,1)S(1)}, bf16[256,2,8,128]{3,2,1,0:T(8,128)(2,1)S(1)}, u32[]{:S(2)}, u32[]{:S(2)}) collective-permute-start(bf16[256,2,8,128]{3,2,1,0:T(8,128)(2,1)S(1)} %slice.156), channel_id=1, source_target_pairs={{0,64},{1,65},{2,66},{3,67},{4,68},{5,69},{6,70},{7,71},{8,72},{9,... | collective-permute-start | bytes 3145736 | tf_op jit(solution)/shard_map/ppermute | solution.py:13
where the time goes:
time: 436 us; the launch traced here: 428 us
  waiting for transfers between devices  136 us (31%)
  local copies, waits for them, and re-layouts  119 us (27%)
  matrix products  108 us (25%)
  other arithmetic  43.1 us (10%)
  starting transfers between devices  21.4 us (5%)
    all_to_all x1, waiting for transfers between devices, local(): lax.all_to_all(channelised, 'grp', split_axis=2, concat_axis=0, tiled=True)  62.7 us
    all_to_all x1, waiting for transfers between devices, local(): lax.all_to_all(formed.reshape(per_target, 2, beam_count, channel_spectra)...  52.8 us
    dot_general x1, matrix products, local(): jnp.einsum('asp,pj->ajs', weighted, dft_cols, preferred_element_type=jnp....  44.7 us
    gather x2, local copies, waits for them, and re-layouts, local(): jnp.take(beam_weights, antenna_of_row, axis=3)  32.6 us
    ppermute x2, waiting for transfers between devices, shifted(): lax.ppermute(value, axis, [(source, source + steps) for source in range(l...  20 us
    unnamed x10, local copies, waits for them, and re-layouts  17.5 us
    dot_general x1, matrix products, dedisperse(): jnp.einsum('cbml,lk->cbmk', blocks[:, 1], forward_imag, preferred_element...  13.9 us
    dot_general x1, matrix products, dedisperse(): jnp.einsum('cbmk,kn->cbmn', filtered_imag, inverse_imag, preferred_elemen...  13.5 us
  transfers between devices with their start and end apart: 4, of which 4 were waited for; matrix products, arithmetic and copies ran while one was open for 16% of the time, Pallas kernels for 0%

commit v1 on v0

--- a/solution.py
+++ b/solution.py
@@ -147,12 +147,20 @@
     beam_real = with_real[:, :beam_count] - with_imag[:, beam_count:]
     beam_imag = with_imag[:, :beam_count] + with_real[:, beam_count:]
     formed = jnp.stack([beam_real, beam_imag], axis=1).astype(jnp.bfloat16)
-    arrival_buffer = lax.all_to_all(
-        formed.reshape(per_target, 2, beam_count, channel_spectra),
-        "grp",
-        split_axis=2,
-        concat_axis=0,
-        tiled=True,
+    arrival_buffer = jnp.concatenate(
+        lax.all_to_all(
+            jnp.stack(
+                jnp.split(
+                    formed.reshape(per_target, 2, beam_count, channel_spectra),
+                    lax.axis_size("grp"),
+                    axis=2,
+                )
+            ),
+            "grp",
+            0,
+            0,
+        ),
+        axis=0,
     )
     leading = shifted(arrival_buffer[:, :, :, channel_spectra - DFT_LEN // 2 :], "section", 1)
     result = dedisperse(arrival_buffer, leading, beam_delay, tables, channels)

time: 436 us -> 470 us (1.078)
  other arithmetic: 43.1 us -> 83.3 us
  local copies, waits for them, and re-layouts: 119 us -> 112 us
    unnamed x1 -> x64, other arithmetic: 0.01 us -> 39.9 us
    another operation x1 -> x0, local copies, waits for them, and re-layouts: 5.25 us -> none  [local(): formed = jnp.stack([beam_real, beam_imag], axis=1).astype(jnp.bfloat16)]
  transfers between devices with their start and end apart: 4 -> 4, of which waited for: 4 -> 4; matrix products, arithmetic and copies ran while one was open for 16% -> 15% of each run, Pallas kernels for 0% -> 0%
where the time goes in v1:
time: 470 us; the launch traced here: 461 us
  waiting for transfers between devices  135 us (29%)
  local copies, waits for them, and re-layouts  112 us (24%)
  matrix products  108 us (23%)
  other arithmetic  83.3 us (18%)
  starting transfers between devices  21.6 us (5%)
    all_to_all x1, waiting for transfers between devices, local(): lax.all_to_all(channelised, 'grp', split_axis=2, concat_axis=0, tiled=True)  62.7 us
    all_to_all x1, waiting for transfers between devices, local(): lax.all_to_all(jnp.stack(jnp.split(formed.reshape(per_target, 2, beam_cou...  52.8 us
    dot_general x1, matrix products, local(): jnp.einsum('asp,pj->ajs', weighted, dft_cols, preferred_element_type=jnp....  44.7 us
    unnamed x64, other arithmetic  39.9 us
    gather x2, local copies, waits for them, and re-layouts, local(): jnp.take(beam_weights, antenna_of_row, axis=3)  32.6 us
    ppermute x2, waiting for transfers between devices, shifted(): lax.ppermute(value, axis, [(source, source + steps) for source in range(l...  19.8 us
    unnamed x10, local copies, waits for them, and re-layouts  17.5 us
    dot_general x1, matrix products, dedisperse(): jnp.einsum('cbml,lk->cbmk', blocks[:, 1], forward_imag, preferred_element...  13.9 us
  transfers between devices with their start and end apart: 4, of which 4 were waited for; matrix products, arithmetic and copies ran while one was open for 15% of the time, Pallas kernels for 0%

profile of v1, /device:TPU:70, one launch (start us, length us, event | category | flops | bytes accessed | tf_op | source)
XLA Modules:
  0.0 461.2 jit_solution(2829862141855970004)
XLA Ops:
  9.2 7.2 %pad_maximum_fusion = bf16[16,265728]{1,0:T(8,128)(2,1)} fusion(bf16[16,262144]{1,0:T(8,128)(2,1)} %param.5, bf16[16,3584]{1,0:T(8,128)(2,1)S(1)} %collective-permute-done), kind=kLoop, calls=%fused_computation.129 | loop fusion | flops 17006592 | bytes 17006592 | tf_op jit(solution)/shard_map/concatenate | solution.py:111
  16.4 12.4 %reshape.191 = bf16[16,519,512]{2,1,0:T(8,128)(2,1)} reshape(bf16[16,265728]{1,0:T(8,128)(2,1)} %pad_maximum_fusion) | data formatting | bytes 17006592 | tf_op jit(solution)/shard_map/reshape | solution.py:111
  28.7 44.7 %convert_bitcast_fusion = bf16[1,16,512,512]{3,2,1,0:T(8,128)(2,1)} fusion(bf16[16,519,512]{2,1,0:T(8,128)(2,1)} %reshape.191, f32[512]{0:T(512)S(1)} %bitcast.221, f32[512]{0:T(512)S(1)} %bitcast.222, f32[512]{0:T(512)S(1)} %bitcast.216, f32[512]{0:T(512)S(1)} %bitcast.217, f32[512]{0:T(512)S(1)} %bitcast.218, f32[512]{0:T(512)S(1)} %bitcast.219, ...), kind=kOutput, calls=%fused_computation.134 | convolution fusion | flops 4399824896 | bytes 76038144 | tf_op jit(solution)/shard_map/asp,pj->ajs/dot_general | solution.py:123
  73.4 11.4 %copy.32 = bf16[1,16,512,512]{3,1,0,2:T(8,128)(2,1)} copy(bf16[1,16,512,512]{3,2,1,0:T(8,128)(2,1)} %convert_bitcast_fusion) | data formatting | bytes 16777216 | tf_op jit(solution)/shard_map/broadcast_in_dim | solution.py:123
  84.8 9.8 %all-to-all-start = ((bf16[1,16,512,512]{3,1,0,2:T(8,128)(2,1)}), bf16[1,16,512,512]{3,1,0,2:T(8,128)(2,1)}, u32[]{:S(2)}, u32[]{:S(2)}) async-start(bf16[1,16,512,512]{3,1,0,2:T(8,128)(2,1)} %copy.32), calls=%async_computation | async-start | bytes 16777216 | tf_op jit(solution)/shard_map/all_to_all | solution.py:131
  94.6 14.8 %copy.30 = bf16[4,2,512,1024]{2,0,3,1:T(4,128)(2,1)} copy(bf16[4,2,512,1024]{3,2,1,0:T(8,128)(2,1)} %param.7) | data formatting | bytes 16777216 | tf_op args[2]
  109.4 19.0 %gather_fusion = bf16[1024,4,2,512]{3,1,2,0:T(4,128)(2,1)} fusion(bf16[4,2,512,1024]{2,0,3,1:T(4,128)(2,1)} %copy.30, s32[1024]{0:T(1024)S(1)} %fusion.113), kind=kCustom, calls=%fused_computation | custom fusion | bytes 16781312 | tf_op jit(solution)/shard_map/jit(_take)/gather | solution.py:127
  128.4 13.7 %copy.31 = bf16[4,2,512,1024]{3,2,1,0:T(8,128)(2,1)} copy(bf16[4,2,512,1024]{2,0,1,3:T(4,128)(2,1)} %bitcast.206) | data formatting | bytes 16777216 | tf_op jit(solution)/shard_map/jit(_take)/gather | solution.py:127
  142.1 7.3 %bitcast_select_fusion = bf16[4,1024,1024]{2,1,0:T(8,128)(2,1)} fusion(bf16[4,2,512,1024]{3,2,1,0:T(8,128)(2,1)} %copy.31, pred[1024]{0:T(1024)(128)(4,1)S(1)} %compare_and_fusion), kind=kLoop, calls=%fused_computation.131 | loop fusion | flops 4194304 | bytes 16778240 | tf_op jit(solution)/shard_map/jit(_take)/select_n | solution.py:127
  149.4 62.7 %all-to-all-done = bf16[1,16,512,512]{3,1,0,2:T(8,128)(2,1)} async-done(((bf16[1,16,512,512]{3,1,0,2:T(8,128)(2,1)}), bf16[1,16,512,512]{3,1,0,2:T(8,128)(2,1)}, u32[]{:S(2)}, u32[]{:S(2)}) %all-to-all-start) | async-done | bytes 8388640 | tf_op jit(solution)/shard_map/all_to_all | solution.py:131
  212.1 8.3 %copy.33 = bf16[1,16,64,8,512]{4,1,2,3,0:T(8,128)(2,1)} copy(bf16[1,16,64,8,512]{4,1,3,2,0:T(8,128)(2,1)} %bitcast.13) | data formatting | bytes 16777216 | tf_op jit(solution)/shard_map/all_to_all | solution.py:131
  220.5 8.3 %fusion.12 = f32[4,1024,1,512]{3,1,0,2:T(8,128)S(1)} fusion(bf16[4,1024,1024]{2,1,0:T(8,128)(2,1)} %bitcast_select_fusion, bf16[1,1024,8,512]{3,1,2,0:T(8,128)(2,1)} %bitcast.213), kind=kOutput, calls=%fused_computation.156 | convolution fusion | flops 4294967296 | bytes 20971520 | tf_op jit(solution)/shard_map/cba,hacs->cbhs/dot_general | solution.py:135
  228.8 9.0 %fusion.13 = f32[4,1024,1,512]{3,1,0,2:T(8,128)} fusion(bf16[4,1024,1024]{2,1,0:T(8,128)(2,1)S(1)} %bitcast.212, bf16[1,1024,8,512]{3,1,2,0:T(8,128)(2,1)} %bitcast.214), kind=kOutput, calls=%fused_computation.157 | convolution fusion | flops 4294967296 | bytes 20971520 | tf_op jit(solution)/shard_map/cba,hacs->cbhs/dot_general | solution.py:141
  282.6 9.0 %all-to-all-start.1 = ((bf16[64,4,2,8,512]{4,3,1,2,0:T(8,128)(2,1)}), bf16[64,4,2,8,512]{4,3,1,2,0:T(8,128)(2,1)}, u32[]{:S(2)}, u32[]{:S(2)}) async-start(bf16[64,4,2,8,512]{4,3,1,2,0:T(8,128)(2,1)} %constant_dynamic-update-slice_fusion), calls=%async_computation.1 | async-start | bytes 8388608 | tf_op jit(solution)/shard_map/all_to_all | solution.py:151
  293.8 52.8 %all-to-all-done.1 = bf16[64,4,2,8,512]{4,3,1,2,0:T(8,128)(2,1)} async-done(((bf16[64,4,2,8,512]{4,3,1,2,0:T(8,128)(2,1)}), bf16[64,4,2,8,512]{4,3,1,2,0:T(8,128)(2,1)}, u32[]{:S(2)}, u32[]{:S(2)}) %all-to-all-start.1) | async-done | bytes 4194336 | tf_op jit(solution)/shard_map/all_to_all | solution.py:151
  351.2 7.4 %fusion.18 = (f32[256,8,256]{2,0,1:T(8,128)S(1)}, f32[256,8,256]{2,0,1:T(8,128)S(1)}) fusion(f32[256]{0:T(256)S(1)} %get-tuple-element.26, f32[256]{0:T(256)S(1)} %get-tuple-element.25, f32[256,8]{0,1:T(8,128)S(1)} %broadcast_multiply_fusion), kind=kLoop, calls=%fused_computation.163 | loop fusion | flops 1048576 | bytes 4204544 | tf_op jit(solution)/shard_map/cos | solution.py:65
  358.6 19.0 %collective-permute-done.1 = bf16[256,2,8,128]{3,2,1,0:T(8,128)(2,1)S(1)} collective-permute-done((bf16[256,2,8,128]{3,2,1,0:T(8,128)(2,1)S(1)}, bf16[256,2,8,128]{3,2,1,0:T(8,128)(2,1)S(1)}, u32[]{:S(2)}, u32[]{:S(2)}) %collective-permute-start.1) | collective-permute-done | bytes 1048608 | tf_op jit(solution)/shard_map/ppermute | solution.py:13
  387.5 8.1 %fusion.3 = f32[256,8,4,512]{3,0,2,1:T(8,128)} fusion(bf16[256,2,8,4,256]{4,0,3,2,1:T(8,128)(2,1)S(1)} %copy_dynamic-update-slice_fusion, bf16[256,256]{1,0:T(8,128)(2,1)S(1)} %fusion.112, bf16[256,256]{1,0:T(8,128)(2,1)S(1)} %get-tuple-element.24), kind=kOutput, calls=%fused_computation.141 | convolution fusion | flops 2148007936 | bytes 21233664 | tf_op jit(solution)/shard_map/cbml,lk->cbmk/dot_general | solution.py:80
  395.6 13.9 %convolution_add_fusion = f32[256,8,4,512]{3,0,2,1:T(8,128)} fusion(f32[256,8,4,512]{3,0,2,1:T(8,128)} %fusion.3, bf16[256,2,8,4,256]{4,0,3,2,1:T(8,128)(2,1)S(1)} %copy_dynamic-update-slice_fusion, bf16[256,256]{1,0:T(8,128)(2,1)S(1)} %get-tuple-element.24, bf16[256,256]{1,0:T(8,128)(2,1)S(1)} %get-tuple-element.23), kind=kOutput, calls=%fused_computation.128 | convolution fusion | flops 2152202240 | bytes 38010880 | tf_op jit(solution)/shard_map/cbml,lk->cbmk/dot_general | solution.py:82
  409.4 10.9 %fusion.1 = f32[256,8,4,256]{0,3,2,1:T(8,128)} fusion(f32[256,8,4,512]{3,0,2,1:T(8,128)} %convolution_add_fusion, f32[256,8,256]{2,0,1:T(8,128)S(1)} %get-tuple-element.22, f32[256,8,256]{2,0,1:T(8,128)S(1)} %get-tuple-element.21, bf16[256,128]{1,0:T(8,128)(2,1)S(1)} %get-tuple-element.12, bf16[256,128]{1,0:T(8,128)(2,1)S(1)} %slice.163), kind=kOutput, calls=%fused_computation.137 | convolution fusion | flops 1082392576 | bytes 29491200 | tf_op jit(solution)/shard_map/cbmk,kn->cbmn/dot_general | solution.py:90
  420.3 13.5 %fusion.14 = f32[256,8,4,256]{0,3,2,1:T(8,128)} fusion(f32[256,8,4,256]{0,3,2,1:T(8,128)} %fusion.1, f32[256,8,4,512]{3,0,2,1:T(8,128)} %convolution_add_fusion, f32[256,8,256]{2,0,1:T(8,128)S(1)} %get-tuple-element.22, f32[256,8,256]{2,0,1:T(8,128)S(1)} %get-tuple-element.21, bf16[256,128]{1,0:T(8,128)(2,1)S(1)} %slice.163, ...), kind=kOutput, calls=%fused_computation.158 | convolution fusion | flops 1084489728 | bytes 37879808 | tf_op jit(solution)/shard_map/cbmk,kn->cbmn/dot_general | solution.py:92
  433.8 7.7 %fusion.142 = (f32[256,8,4,128]{0,3,2,1:T(8,128)}, f32[256,8,4,128]{0,3,2,1:T(8,128)}) fusion(f32[256,8,4,256]{0,3,2,1:T(8,128)} %fusion.14), kind=kLoop, calls=%fused_computation.389 | loop fusion | bytes 16777216 | tf_op jit(solution)/shard_map/slice | solution.py:93
  441.5 5.6 %copy.39 = f32[256,1,8,512]{3,2,1,0:T(8,128)} copy(f32[256,1,8,512]{0,3,2,1:T(8,128)} %bitcast.210) | data formatting | bytes 8388608 | tf_op jit(solution)/shard_map/stack;reshape | solution.py:95
  452.6 8.1 %pad_maximum_fusion.1 = f32[256,2,8,512]{3,2,1,0:T(8,128)} fusion(f32[256,1,8,512]{3,2,1,0:T(8,128)} %copy.40, f32[256,1,8,512]{3,2,1,0:T(8,128)} %copy.39), kind=kLoop, calls=%fused_computation.130 | loop fusion | flops 2097152 | bytes 16777216 | tf_op jit(solution)/shard_map/stack | solution.py:95
  (99 shorter events, 76.0 us)
Async XLA Ops:
  0.9 8.3 %collective-permute-start = (bf16[16,3584]{1,0:T(8,128)(2,1)S(1)}, bf16[16,3584]{1,0:T(8,128)(2,1)S(1)}, u32[]{:S(2)}, u32[]{:S(2)}) collective-permute-start(bf16[16,3584]{1,0:T(8,128)(2,1)S(1)} %slice.107), channel_id=1, source_target_pairs={{0,64},{1,65},{2,66},{3,67},{4,68},{5,69},{6,70},{7,71},{8,72},{9,... | collective-permute-start | bytes 344072 | tf_op jit(solution)/shard_map/ppermute | solution.py:13
  84.8 127.4 %all-to-all-start = ((bf16[1,16,512,512]{3,1,0,2:T(8,128)(2,1)}), bf16[1,16,512,512]{3,1,0,2:T(8,128)(2,1)}, u32[]{:S(2)}, u32[]{:S(2)}) async-start(bf16[1,16,512,512]{3,1,0,2:T(8,128)(2,1)} %copy.32), calls=%async_computation | async-start | bytes 16777216 | tf_op jit(solution)/shard_map/all_to_all | solution.py:131
  94.6 14.8 %copy-start = (s32[1024]{0:T(1024)S(1)}, s32[1024]{0:T(1024)}, u32[]{:S(2)}) copy-start(s32[1024]{0:T(1024)} %param.8) | copy-start | bytes 12292
  212.1 16.6 %slice-start = ((s8[8388608]{0:T(1024)(128)(4,1)}), s8[4194304]{0:T(1024)(128)(4,1)S(1)}, s32[]{:S(2)}) async-start(s8[8388608]{0:T(1024)(128)(4,1)} %bitcast.211), calls=%async_computation.2 | async-start | bytes 8388608
  220.5 8.3 %slice-start.1 = ((s8[8388608]{0:T(1024)(128)(4,1)}), s8[4194304]{0:T(1024)(128)(4,1)S(1)}, s32[]{:S(2)}) async-start(s8[8388608]{0:T(1024)(128)(4,1)} %bitcast.211), calls=%async_computation.3 | async-start | bytes 8388608
  282.6 64.0 %all-to-all-start.1 = ((bf16[64,4,2,8,512]{4,3,1,2,0:T(8,128)(2,1)}), bf16[64,4,2,8,512]{4,3,1,2,0:T(8,128)(2,1)}, u32[]{:S(2)}, u32[]{:S(2)}) async-start(bf16[64,4,2,8,512]{4,3,1,2,0:T(8,128)(2,1)} %constant_dynamic-update-slice_fusion), calls=%async_computation.1 | async-start | bytes 8388608 | tf_op jit(solution)/shard_map/all_to_all | solution.py:151
  293.8 57.3 %copy-start.1 = (s32[8]{0:T(128)S(1)}, s32[8]{0:T(128)}, u32[]{:S(2)}) copy-start(s32[8]{0:T(128)} %param.9) | copy-start | bytes 100
  349.6 28.0 %collective-permute-start.1 = (bf16[256,2,8,128]{3,2,1,0:T(8,128)(2,1)S(1)}, bf16[256,2,8,128]{3,2,1,0:T(8,128)(2,1)S(1)}, u32[]{:S(2)}, u32[]{:S(2)}) collective-permute-start(bf16[256,2,8,128]{3,2,1,0:T(8,128)(2,1)S(1)} %slice.156), channel_id=1, source_target_pairs={{0,64},{1,65},{2,66},{3,67},{4,68},{5,69},{6,70},{7,71},{8,72},{9,... | collective-permute-start | bytes 3145736 | tf_op jit(solution)/shard_map/ppermute | solution.py:13
